TPU v7x, 32 devices: a whole 2x2x4 slice. The times are simulated.
32 devices in a mesh: owner: 8 (over y, x, core), rows: 4 (over z).
Axes of the slice: x: 2, y: 2, z: 4, core: 2. Of those that a mesh axis runs over, the one named last changes fastest.
Arguments:
- w_down: float32 [64, 1024, 2048], P('owner', None, 'rows'), may hold values from -0.1875 to 0.1875
- router_weight: float32 [2048, 64], P('rows', 'owner'), may hold values from -0.125 to 0.125
- router_gain: float32 [2048], P('rows'), may hold values from 0.25 to 1.75
Outputs:
- serve_down: bfloat16 [64, 2048, 1024], P('owner')
- serve_router: bfloat16 [2048, 64], replicated
All inputs are finite; a program needn't handle non-finite values.
Results may differ from a plain program's by a relative error of at most 0.001.
Values may be sent and summed in bfloat16 or wider, within the bound.
A program may use at most 128 MiB of HBM per device.

v0:
```python
import jax
import jax.numpy as jnp
from jax import lax
from jax.sharding import PartitionSpec as P


def shards(w_down, router_weight, router_gain):
    narrow_down = w_down.astype(jnp.bfloat16)
    serve_down = lax.all_gather(narrow_down, "rows", axis=2, tiled=True)
    serve_down = jnp.transpose(serve_down, (0, 2, 1))
    part_router = (router_weight * router_gain[:, None]).astype(jnp.bfloat16)
    row_router = lax.all_gather(part_router, "rows", axis=0, tiled=True)
    serve_router = lax.all_gather(row_router, "owner", axis=1, tiled=True)
    return (serve_down, serve_router)


def solution(mesh):
    in_specs = (P("owner", None, "rows"), P("rows", "owner"), P("rows"))
    out_specs = (P("owner", None, None), P())
    return jax.shard_map(shards, mesh=mesh, in_specs=in_specs, out_specs=out_specs, check_vma=False)
```

profile of v0, /device:TPU:0, one launch (start us, length us, event | category | flops | bytes accessed | tf_op | source)
XLA Modules:
  0.0 615.9 jit_solution(6089209621411756597)
XLA Ops:
  7.2 0.0 copy-start
  7.2 0.0 copy-start.1
  7.2 0.0 all-gather.2.cloned.1.call-start
  7.2 13.6 %copy.5 = bf16[8,1024,512]{1,2,0:T(8,128)(2,1)} copy(f32[8,1024,512]{2,1,0:T(8,128)} %param.3) | data formatting | bytes 25165824 | tf_op args[0]
  20.8 0.0 all-gather.2.cloned.1.call-update
  20.8 0.0 copy-done
  20.8 0.0 copy-done.1
  20.9 14.8 %all_gather.10 = bf16[2048,8]{0,1:T(8,128)(2,1)S(1)} all-gather(bf16[512,8]{0,1:T(8,128)(2,1)S(1)} %multiply_convert_fusion), channel_id=1, replica_groups=mesh['owner'=8,'rows'=4] {'rows'}, dimensions={0}, use_global_device_ids=true | all-gather | bytes 40960 | tf_op jit(solution)/shard_map/all_gather | solution.py:12
  35.7 9.3 %all_gather.11 = bf16[2048,64]{0,1:T(8,128)(2,1)S(1)} all-gather(bf16[2048,8]{0,1:T(8,128)(2,1)S(1)} %all_gather.10), channel_id=1, replica_groups=mesh['owner'=8,'rows'=4] {'owner'}, dimensions={1}, use_global_device_ids=true | all-gather | bytes 294912 | tf_op jit(solution)/shard_map/all_gather | solution.py:13
  45.0 540.1 %all-gather.2.cloned.1.call-done = bf16[8,1024,2048]{1,2,0:T(8,128)(2,1)} async-done(((bf16[8,1024,512]{1,2,0:T(8,128)(2,1)}), bf16[8,1024,2048]{1,2,0:T(8,128)(2,1)}) %all-gather.2.cloned.1.call-update) | async-done | bytes 33554448 | tf_op jit(solution)/shard_map/all_gather | solution.py:9
  585.1 23.2 %copy.8 = bf16[8,2048,1024]{2,1,0:T(8,128)(2,1)} copy(bf16[8,2048,1024]{2,1,0:T(8,128)(2,1)} %bitcast.1) | data formatting | bytes 67108864
  608.3 0.7 copy.9
  (1 shorter events, 0.0 us)
Async XLA Ops:
  7.2 13.7 %copy-start = (f32[512,8]{0,1:T(8,128)S(1)}, f32[512,8]{0,1:T(8,128)}, u32[]{:S(2)}) copy-start(f32[512,8]{0,1:T(8,128)} %param.4) | copy-start | bytes 49156
  7.2 13.7 %copy-start.1 = (f32[512]{0:T(512)S(1)}, f32[512]{0:T(512)}, u32[]{:S(2)}) copy-start(f32[512]{0:T(512)} %param.5) | copy-start | bytes 6148
  7.2 577.9 %all-gather.2.cloned.1.call-start = ((), (), s32[]{:S(2)}) async-start(), calls=%async_computation | async-start | bytes 41943040 | tf_op jit(solution)/shard_map/all_gather | solution.py:9
Sparse Core Ops, SparseCore 0:
  20.9 564.0 all-gather.1
where the time goes:
time: 616 us
  waiting for transfers between devices  540 us (88%)
  local copies, waits for them, and re-layouts  37.5 us (6%)
  blocking collectives  24.1 us (4%)
  between operations  14.1 us (2%)
    all_gather x1, waiting for transfers between devices, shards(): serve_down = lax.all_gather(narrow_down, 'rows', axis=2, tiled=True)  540 us
    unnamed x7, local copies, waits for them, and re-layouts  37.5 us
    all_gather x1, blocking collectives, shards(): row_router = lax.all_gather(part_router, 'rows', axis=0, tiled=True)  14.8 us
  transfers between devices with their start and end apart: 1, of which 1 were waited for; matrix products, arithmetic and copies ran while one was open for 0% of the time, Pallas kernels for 0%

commit v1 on v0

--- a/solution.py
+++ b/solution.py
@@ -6,7 +6,8 @@
 
 def shards(w_down, router_weight, router_gain):
     narrow_down = w_down.astype(jnp.bfloat16)
-    serve_down = lax.all_gather(narrow_down, "rows", axis=2, tiled=True)
+    pieces = lax.all_gather(narrow_down, "rows")
+    serve_down = jnp.concatenate(pieces, axis=2)
     serve_down = jnp.transpose(serve_down, (0, 2, 1))
     part_router = (router_weight * router_gain[:, None]).astype(jnp.bfloat16)
     row_router = lax.all_gather(part_router, "rows", axis=0, tiled=True)

time: 616 us -> 631 us (1.024)
  other arithmetic: 0.01 us -> 8.98 us
    reshape x0 -> x1, local copies, waits for them, and re-layouts: none -> 42 us  [shards(): serve_down = jnp.concatenate(pieces, axis=2)]
    unnamed x7 -> x5, local copies, waits for them, and re-layouts: 37.5 us -> 0.71 us
    convert_element_type x0 -> x1, other arithmetic: none -> 8.98 us  [shards(): narrow_down = w_down.astype(jnp.bfloat16)]
where the time goes in v1:
time: 631 us; the launch traced here: 630 us
  waiting for transfers between devices  540 us (86%)
  local copies, waits for them, and re-layouts  42.7 us (7%)
  blocking collectives  24.1 us (4%)
  between operations  14.1 us (2%)
  other arithmetic  8.98 us (1%)
    all_gather x1, waiting for transfers between devices, shards(): pieces = lax.all_gather(narrow_down, 'rows')  540 us
    reshape x1, local copies, waits for them, and re-layouts, shards(): serve_down = jnp.concatenate(pieces, axis=2)  42 us
    all_gather x1, blocking collectives, shards(): row_router = lax.all_gather(part_router, 'rows', axis=0, tiled=True)  14.8 us
  transfers between devices with their start and end apart: 1, of which 1 were waited for; matrix products, arithmetic and copies ran while one was open for 0% of the time, Pallas kernels for 0%

profile of v1, /device:TPU:0, one launch (start us, length us, event | category | flops | bytes accessed | tf_op | source)
XLA Modules:
  0.0 630.0 jit_solution(4098347636613212321)
XLA Ops:
  7.2 0.0 copy-start
  7.2 0.0 copy-start.1
  7.2 0.0 all-gather.3.cloned.1.call-start
  7.2 9.0 %convert_element_type.6 = bf16[8,1024,512]{2,1,0:T(8,128)(2,1)} convert(f32[8,1024,512]{2,1,0:T(8,128)} %param.3) | non-fusion elementwise | flops 4194304 | bytes 25165824 | tf_op jit(solution)/shard_map/convert_element_type | solution.py:8
  16.2 0.0 all-gather.3.cloned.1.call-update
  16.2 0.0 copy-done
  16.2 0.0 copy-done.1
  16.3 14.8 %all_gather.14 = bf16[2048,8]{0,1:T(8,128)(2,1)S(1)} all-gather(bf16[512,8]{0,1:T(8,128)(2,1)S(1)} %multiply_convert_fusion), channel_id=1, replica_groups=mesh['owner'=8,'rows'=4] {'rows'}, dimensions={0}, use_global_device_ids=true | all-gather | bytes 40960 | tf_op jit(solution)/shard_map/all_gather | solution.py:13
  31.1 9.3 %all_gather.15 = bf16[2048,64]{0,1:T(8,128)(2,1)S(1)} all-gather(bf16[2048,8]{0,1:T(8,128)(2,1)S(1)} %all_gather.14), channel_id=1, replica_groups=mesh['owner'=8,'rows'=4] {'owner'}, dimensions={1}, use_global_device_ids=true | all-gather | bytes 294912 | tf_op jit(solution)/shard_map/all_gather | solution.py:14
  40.4 540.1 %all-gather.3.cloned.1.call-done = bf16[32,1024,512]{2,1,0:T(8,128)(2,1)} async-done(((bf16[8,1024,512]{2,1,0:T(8,128)(2,1)}), bf16[32,1024,512]{2,1,0:T(8,128)(2,1)}) %all-gather.3.cloned.1.call-update) | async-done | bytes 33554448 | tf_op jit(solution)/shard_map/all_gather | solution.py:9
  580.5 42.0 %copy.6 = bf16[8,1024,4,512]{1,3,2,0:T(8,128)(2,1)} copy(bf16[8,1024,4,512]{3,1,0,2:T(8,128)(2,1)} %bitcast.6) | data formatting | bytes 67108864 | tf_op jit(solution)/shard_map/reshape | solution.py:10
  622.5 0.7 copy.8
  (1 shorter events, 0.0 us)
Async XLA Ops:
  7.2 9.1 %copy-start = (f32[512,8]{0,1:T(8,128)S(1)}, f32[512,8]{0,1:T(8,128)}, u32[]{:S(2)}) copy-start(f32[512,8]{0,1:T(8,128)} %param.4) | copy-start | bytes 49156
  7.2 9.1 %copy-start.1 = (f32[512]{0:T(512)S(1)}, f32[512]{0:T(512)}, u32[]{:S(2)}) copy-start(f32[512]{0:T(512)} %param.5) | copy-start | bytes 6148
  7.2 573.3 %all-gather.3.cloned.1.call-start = ((), (), s32[]{:S(2)}) async-start(), calls=%async_computation | async-start | bytes 41943040 | tf_op jit(solution)/shard_map/all_gather | solution.py:9
Sparse Core Ops, SparseCore 0:
  16.4 564.0 all-gather.2
